TPU v7x, 32 devices: a whole 2x2x4 slice. The times are simulated.
32 devices in a mesh: groups: 2 (over y), chan: 4 (over z), dop: 2 (over x), sub: 2 (over core).
Axes of the slice: x: 2, y: 2, z: 4, core: 2. Of those that a mesh axis runs over, the one named last changes fastest.
Arguments:
- power: bfloat16 [2, 512, 128, 1024], P(None, ('groups', 'chan', 'sub'), 'dop'), parts along dimension 1, may hold values from 0.049804688 to 20
- window: int32 [4, 2], P('groups'), parts along dimension 0, may hold values from 1 to 32, as said below
- calib_index: int32 [4, 32], P('groups', ('chan', 'sub')), parts along dimension 0, may hold values from 0 to 15
- calib_table: float32 [16], replicated, may hold values from 0.5 to 8
Outputs:
- test_ratio: float32 [2, 256, 1024], P(None, ('groups', 'dop'), ('chan', 'sub')), parts along dimension 1
There are 2 independent parts, one for each index of `groups`. A program takes and returns all parts, laid end to end along the dimension named above; an argument that names none is the same for every part. Nothing has to cross between parts.
Inputs may be any that keep to these rules, and one draw needn't show every extreme that they name: window[c, 0] is the guard count, from 1 to 8; window[c, 1] is the reach, from 16 to 32; interval 0 has reach 32.
All inputs are finite; a program needn't handle non-finite values.
Results may differ from a plain program's by a relative error of at most 0.0003.
Values sent between devices are 32-bit elements; how exact they have to be, the bound alone decides.
A program may use at most 64 MiB of HBM per device.

v0:
```python
import jax
import jax.numpy as jnp
from jax import lax
from jax.sharding import PartitionSpec as P

HALO = 32
CALIB = 32


def extended(block, sides, width):
    for axis, dim in sides:
        count = lax.axis_size(axis)
        forward = [(i, i + 1) for i in range(count - 1)]
        backward = [(target, source) for source, target in forward]
        low = lax.ppermute(
            lax.slice_in_dim(block, block.shape[dim] - width, None, axis=dim), axis, forward
        )
        high = lax.ppermute(lax.slice_in_dim(block, 0, width, axis=dim), axis, backward)
        block = jnp.concatenate([low, block, high], axis=dim)
    return block


def body(power, window, calib_index, calib_table):
    partial_sum = jnp.sum(power, axis=1, dtype=jnp.float32)
    strip = lax.psum_scatter(partial_sum, ("chan", "sub"), scatter_dimension=2, tiled=True)
    cells = strip.shape[2]
    padded = extended(strip, ((("chan", "sub"), 2),), HALO)
    guard = window[:, 0]
    reach = window[:, 1]
    source = jnp.arange(cells + 2 * HALO, dtype=jnp.int32)[:, None]
    target = jnp.arange(cells, dtype=jnp.int32)[None, :]
    distance = jnp.abs(source - HALO - target)
    band_matrix = (
        (distance[None, :, :] > guard[:, None, None])
        & (distance[None, :, :] <= reach[:, None, None])
    ).astype(jnp.float32)
    total = jnp.einsum("cdj,cji->cdi", padded, band_matrix, precision=lax.Precision.HIGHEST)
    noise = total / (2.0 * (reach - guard).astype(jnp.float32))[:, None, None]
    levels = jnp.arange(calib_table.shape[0], dtype=jnp.int32)
    onehot = (calib_index[:, :, None] == levels[None, None, :]).astype(jnp.float32)
    block_scale = jnp.sum(onehot * calib_table[None, None, :], axis=-1)
    intervals = block_scale.shape[0]
    blocks = block_scale.shape[1]
    scale = jnp.broadcast_to(block_scale[:, :, None], (intervals, blocks, CALIB)).reshape(
        intervals, cells
    )
    return strip / (scale[:, None, :] * noise)


def solution(mesh):
    placed = (
        P(None, ("groups", "chan", "sub"), "dop", None),
        P("groups", None),
        P("groups", ("chan", "sub")),
        P(),
    )
    return jax.shard_map(
        body,
        mesh=mesh,
        in_specs=placed,
        out_specs=P(None, ("groups", "dop"), ("chan", "sub")),
        check_vma=False,
    )
```

profile of v0, /device:TPU:1, one launch (start us, length us, event | category | flops | bytes accessed | tf_op | source)
XLA Modules:
  0.0 61.8 jit_solution(2381132366186946309)
XLA Ops:
  6.5 0.0 copy-start
  6.5 0.0 copy-start.2
  6.5 0.0 copy-start.1
  6.5 0.0 reduce-scatter.2.cloned.1.call-start
  6.5 6.3 %convert_reduce_fusion = f32[2,64,1024]{2,1,0:T(8,128)} fusion(bf16[2,32,64,1024]{3,2,1,0:T(8,128)(2,1)} %param.4), kind=kLoop, calls=%fused_computation | loop fusion | flops 8257536 | bytes 8912896 | tf_op jit(solution)/shard_map/reduce_sum | solution.py:24
  12.8 0.0 reduce-scatter.2.cloned.1.call-update
  12.9 0.0 copy-done
  12.9 0.2 slice_reduce_fusion.1
  13.1 0.1 subtract_abs_fusion
  13.2 29.9 %reduce-scatter.2.cloned.1.call-done = f32[2,64,128]{2,1,0:T(8,128)} async-done(((f32[2,64,1024]{2,1,0:T(8,128)}), f32[2,64,128]{2,1,0:T(8,128)}) %reduce-scatter.2.cloned.1.call-update) | async-done | bytes 65552 | tf_op jit(solution)/shard_map/reduce_scatter | solution.py:25
  43.1 1.0 %fusion.14 = (f32[2,64,32]{2,1,0:T(8,128)S(1)}, f32[2,64,32]{2,1,0:T(8,128)S(1)}) fusion(f32[2,64,128]{2,1,0:T(8,128)} %reduce-scatter.2.cloned.1.call-done), kind=kLoop, calls=%fused_computation.23 | loop fusion | bytes 65536 | tf_op jit(solution)/shard_map/slice | solution.py:16
  44.0 5.8 %collective-permute-start.1 = (f32[2,64,32]{2,1,0:T(8,128)S(1)}, f32[2,64,32]{2,1,0:T(8,128)S(1)}, u32[]{:S(2)}, u32[]{:S(2)}) collective-permute-start(f32[2,64,32]{2,1,0:T(8,128)S(1)} %get-tuple-element.8), channel_id=1, source_target_pairs={{1,0},{4,1},{5,4},{8,5},{9,8},{12,9},{13,12},{3,2},{6,3},{7,6},{10... | collective-permute-start | bytes 49160 | tf_op jit(solution)/shard_map/ppermute | solution.py:18
  49.8 1.9 %collective-permute-start = (f32[2,64,32]{2,1,0:T(8,128)S(1)}, f32[2,64,32]{2,1,0:T(8,128)S(1)}, u32[]{:S(2)}, u32[]{:S(2)}) collective-permute-start(f32[2,64,32]{2,1,0:T(8,128)S(1)} %get-tuple-element.7), channel_id=1, source_target_pairs={{0,1},{1,4},{4,5},{5,8},{8,9},{9,12},{12,13},{2,3},{3,6},{6,7},{7,... | collective-permute-start | bytes 49160 | tf_op jit(solution)/shard_map/ppermute | solution.py:15
  51.7 0.0 copy-done.2
  51.7 0.0 copy-done.1
  51.8 0.2 select_reduce_fusion
  51.9 0.1 broadcast_in_dim.2
  52.0 0.1 mul.27
  52.1 0.0 collective-permute-done.1
  52.1 1.0 %collective-permute-done = f32[2,64,32]{2,1,0:T(8,128)S(1)} collective-permute-done((f32[2,64,32]{2,1,0:T(8,128)S(1)}, f32[2,64,32]{2,1,0:T(8,128)S(1)}, u32[]{:S(2)}, u32[]{:S(2)}) %collective-permute-start) | collective-permute-done | bytes 16416 | tf_op jit(solution)/shard_map/ppermute | solution.py:15
  53.0 1.9 %fusion.1 = f32[2,64,128]{2,1,0:T(8,128)} fusion(f32[2,64,128]{2,1,0:T(8,128)} %reduce-scatter.2.cloned.1.call-done, f32[2,64,32]{2,1,0:T(8,128)S(1)} %collective-permute-done.1, f32[2,64,32]{2,1,0:T(8,128)S(1)} %collective-permute-done, s32[192,128]{1,0:T(8,128)S(1)} %subtract_abs_fusion, s32[2]{0:T(128)S(1)} %get-tuple-element.6, ...), kind=kOutput, calls=%fused_computation.3 | convolution fusion | flops 37994496 | bytes 263192 | tf_op jit(solution)/shard_map/cdj,cji->cdi/dot_general | solution.py:37
  (2 shorter events, 0.0 us)
Async XLA Ops:
  6.5 6.3 %copy-start = (s32[2,2]{1,0:T(2,128)S(1)}, s32[2,2]{1,0:T(2,128)}, u32[]{:S(2)}) copy-start(s32[2,2]{1,0:T(2,128)} %param.5) | copy-start | bytes 52
  6.5 45.2 %copy-start.2 = (f32[16]{0:T(128)S(1)}, f32[16]{0:T(128)}, u32[]{:S(2)}) copy-start(f32[16]{0:T(128)} %param.7) | copy-start | bytes 196
  6.5 45.2 %copy-start.1 = (s32[2,4]{1,0:T(2,128)S(1)}, s32[2,4]{1,0:T(2,128)}, u32[]{:S(2)}) copy-start(s32[2,4]{1,0:T(2,128)} %param.6) | copy-start | bytes 100
  6.5 36.5 %reduce-scatter.2.cloned.1.call-start = ((), (), s32[]{:S(2)}) async-start(), calls=%async_computation.1 | async-start | bytes 589824 | tf_op jit(solution)/shard_map/reduce_scatter | solution.py:25
  44.0 8.0 %collective-permute-start.1 = (f32[2,64,32]{2,1,0:T(8,128)S(1)}, f32[2,64,32]{2,1,0:T(8,128)S(1)}, u32[]{:S(2)}, u32[]{:S(2)}) collective-permute-start(f32[2,64,32]{2,1,0:T(8,128)S(1)} %get-tuple-element.8), channel_id=1, source_target_pairs={{1,0},{4,1},{5,4},{8,5},{9,8},{12,9},{13,12},{3,2},{6,3},{7,6},{10... | collective-permute-start | bytes 49160 | tf_op jit(solution)/shard_map/ppermute | solution.py:18
  49.8 3.2 %collective-permute-start = (f32[2,64,32]{2,1,0:T(8,128)S(1)}, f32[2,64,32]{2,1,0:T(8,128)S(1)}, u32[]{:S(2)}, u32[]{:S(2)}) collective-permute-start(f32[2,64,32]{2,1,0:T(8,128)S(1)} %get-tuple-element.7), channel_id=1, source_target_pairs={{0,1},{1,4},{4,5},{5,8},{8,9},{9,12},{12,13},{2,3},{3,6},{6,7},{7,... | collective-permute-start | bytes 49160 | tf_op jit(solution)/shard_map/ppermute | solution.py:15
Sparse Core Ops, SparseCore 0:
  13.0 30.0 reduce-scatter.1
where the time goes:
time: 62.1 us; the launch traced here: 61.8 us
  waiting for transfers between devices  30.9 us (50%)
  between operations  13.5 us (22%)
  starting transfers between devices  7.68 us (12%)
  other arithmetic  6.55 us (11%)
  matrix products  1.87 us (3%)
  local copies, waits for them, and re-layouts  1.33 us (2%)
    reduce_scatter x1, waiting for transfers between devices, body(): lax.psum_scatter(partial_sum, ('chan', 'sub'), scatter_dimension=2, tiled...  29.9 us
    reduce_sum x1, other arithmetic, body(): partial_sum = jnp.sum(power, axis=1, dtype=jnp.float32)  6.29 us
    ppermute x1, starting transfers between devices, extended(): lax.ppermute(lax.slice_in_dim(block, 0, width, axis=dim), axis, backward)  5.76 us
    ppermute x1, starting transfers between devices, extended(): lax.ppermute(lax.slice_in_dim(block, block.shape[dim] - width, None, axis...  1.92 us
    dot_general x1, matrix products, body(): jnp.einsum('cdj,cji->cdi', padded, band_matrix, precision=lax.Precision.H...  1.87 us
  transfers between devices with their start and end apart: 3, of which 2 were waited for; matrix products, arithmetic and copies ran while one was open for 1% of the time, Pallas kernels for 0%

commit v1 on v0

v1 whole, which is shorter than its diff:
```python
import functools

import jax
import jax.numpy as jnp
from jax import lax
from jax.experimental import pallas as pl
from jax.experimental.pallas import tpu as pltpu
from jax.sharding import PartitionSpec as P

HALO = 32
CALIB = 32
LANES = 128
CHUNK_ROWS = 32
MESH = pl.DeviceIdType.MESH


def split_dot(x, band):
    high = x.astype(jnp.bfloat16)
    rest = x - high.astype(jnp.float32)
    mid = rest.astype(jnp.bfloat16)
    low = (rest - mid.astype(jnp.float32)).astype(jnp.bfloat16)
    dot = functools.partial(jnp.dot, preferred_element_type=jnp.float32)
    return dot(high, band) + (dot(mid, band) + dot(low, band))


def kernel(
    chips, cores, window, index, table, power, out,
    raw, part, pair, total, inbox, strip, pack, halo,
    raw_sem, pair_send, pair_recv, z_send, z_recv, halo_send, halo_recv,
):
    chan = lax.axis_index("chan")
    sub = lax.axis_index("sub")
    me = chan * cores + sub
    strips = chips * cores
    other = 1 - sub
    intervals, channels, dops, _ = power.shape
    per = dops // CHUNK_ROWS
    chunks = intervals * per
    cells = LANES
    group = dops * HALO // LANES

    def load(k):
        c, r = k // per, (k % per) * CHUNK_ROWS
        return pltpu.make_async_copy(
            power.at[c, :, pl.ds(r, CHUNK_ROWS), :], raw.at[k], raw_sem.at[k]
        )

    for k in range(chunks):
        load(k).start()

    barrier = pltpu.get_barrier_semaphore()

    @pl.loop(1, strips)
    def _(step):
        peer = lax.rem(me + step, strips)
        pl.semaphore_signal(
            barrier, inc=1, device_id={"chan": peer // cores, "sub": lax.rem(peer, cores)},
            device_id_type=MESH,
        )

    def rows_of(k):
        return pl.ds(k * CHUNK_ROWS, CHUNK_ROWS)

    def channel_sum(k):
        @pl.loop(0, chips)
        def _(j):
            for s in range(cores):
                lanes = pl.ds(pl.multiple_of((j * cores + s) * cells, cells), cells)
                acc = [None] * 2
                for ch in range(channels):
                    x = raw[k, ch, :, lanes].astype(jnp.float32)
                    acc[ch % 2] = x if acc[ch % 2] is None else acc[ch % 2] + x
                part[s, j, rows_of(k), :] = acc[0] + acc[1]

    def to_pair(k):
        return pltpu.make_async_remote_copy(
            src_ref=part.at[other, :, rows_of(k), :],
            dst_ref=pair.at[:, rows_of(k), :],
            send_sem=pair_send.at[k],
            recv_sem=pair_recv.at[k],
            device_id={"sub": other},
            device_id_type=MESH,
        )

    def offset(step):
        return jnp.where(chan < chips // 2, chips - step, step)

    def to_owner(k, step):
        hop = offset(step)
        goal = lax.rem(chan + hop, chips)
        return pltpu.make_async_remote_copy(
            src_ref=total.at[goal, rows_of(k), :],
            dst_ref=inbox.at[hop - 1, rows_of(k), :],
            send_sem=z_send.at[hop - 1, k],
            recv_sem=z_recv.at[hop - 1, k],
            device_id={"chan": goal},
            device_id_type=MESH,
        )

    def from_pair(k):
        to_pair(k).wait_recv()
        for j in range(chips):
            total[j, rows_of(k), :] = part[sub, j, rows_of(k), :] + pair[j, rows_of(k), :]
        for step in range(1, chips):
            to_owner(k, step).start()

    lane = lax.broadcasted_iota(jnp.int32, (group, LANES), 1)

    def to_side(c, side):
        peer = me + (1 if side else -1)
        return pltpu.make_async_remote_copy(
            src_ref=pack.at[side, c],
            dst_ref=halo.at[side, c],
            send_sem=halo_send.at[side, c],
            recv_sem=halo_recv.at[side, c],
            device_id={"chan": peer // cores, "sub": lax.rem(peer, cores)},
            device_id_type=MESH,
        )

    has = (me > 0, me < strips - 1)

    def collect(c):
        for k in range(c * per, (c + 1) * per):
            for hop in range(1, chips):
                to_owner(k, hop).wait_recv()
            value = total[chan, rows_of(k), :]
            for hop in range(1, chips):
                value = value + inbox[hop - 1, rows_of(k), :]
            strip[rows_of(k), :] = value
        for side in range(2):
            packed = None
            for q in range(LANES // HALO):
                x = strip[pl.ds(c * dops + q * group, group), :]
                shift = (q * HALO + side * HALO) % LANES
                x = pltpu.roll(x, shift, 1) if shift else x
                packed = x if packed is None else jnp.where(lane // HALO == q, x, packed)
            pack[side, c] = packed

            @pl.when(has[side])
            def _():
                to_side(c, side).start()

    for k in range(chunks):
        load(k).wait()
        channel_sum(k)
        if k == 0:
            pl.semaphore_wait(barrier, strips - 1)
        to_pair(k).start()
        if k >= 1:
            from_pair(k - 1)
    from_pair(chunks - 1)

    source = lax.broadcasted_iota(jnp.int32, (2 * LANES, LANES), 0)
    target = lax.broadcasted_iota(jnp.int32, (2 * LANES, LANES), 1)
    place = jnp.where(source < LANES + LANES // 2, source, source - 2 * LANES)
    distance = jnp.abs(place - target)
    cell = lax.broadcasted_iota(jnp.int32, (1, LANES), 1)
    full_lane = lax.broadcasted_iota(jnp.int32, (dops, LANES), 1)

    bands, gains = [], []
    for c in range(intervals):
        guard, reach = window[c, 0], window[c, 1]
        bands.append(
            jnp.where((distance > guard) & (distance <= reach), 1.0, 0.0).astype(jnp.bfloat16)
        )
        scale = jnp.zeros((1, LANES), jnp.float32)
        for b in range(cells // CALIB):
            scale = jnp.where(cell // CALIB == b, table[index[c, b]], scale)
        count = jnp.full((1, LANES), 2 * (reach - guard), jnp.int32).astype(jnp.float32)
        gains.append((scale, count))

    for c in range(intervals):
        collect(c)

    for c in range(intervals):
        for side in range(2):
            @pl.when(has[1 - side])
            def _():
                to_side(c, side).wait_recv()

            @pl.when(jnp.logical_not(has[1 - side]))
            def _():
                halo[side, c] = jnp.zeros((group, LANES), jnp.float32)

        wide = []
        for side in range(2):
            pieces = []
            for q in range(LANES // HALO):
                x = halo[side, c]
                shift = (LANES - q * HALO - side * HALO) % LANES
                pieces.append(pltpu.roll(x, shift, 1) if shift else x)
            wide.append(jnp.concatenate(pieces, axis=0))
        edge = jnp.where(full_lane < LANES // 2, wide[0], wide[1])
        mine = strip[pl.ds(c * dops, dops), :]
        window_sum = split_dot(jnp.concatenate([mine, edge], axis=1), bands[c])
        scale, count = gains[c]
        noise = window_sum / count
        out[c] = mine / (scale * noise)

    for k in range(chunks):
        to_pair(k).wait_send()
        for step in range(1, chips):
            to_owner(k, step).wait_send()
    for c in range(intervals):
        for side in range(2):
            @pl.when(has[side])
            def _():
                to_side(c, side).wait_send()


def solution(mesh):
    chips, cores = mesh.shape["chan"], mesh.shape["sub"]

    def body(power, window, calib_index, calib_table):
        intervals, channels, dops, cells = power.shape
        width = cells // (chips * cores)
        rows = intervals * dops
        chunks = rows // CHUNK_ROWS
        group = dops * HALO // LANES
        f32 = jnp.float32
        return pl.pallas_call(
            functools.partial(kernel, chips, cores),
            out_shape=jax.ShapeDtypeStruct((intervals, dops, width), f32),
            in_specs=[pl.BlockSpec(memory_space=pltpu.SMEM)] * 3
            + [pl.BlockSpec(memory_space=pl.ANY)],
            out_specs=pl.BlockSpec(memory_space=pltpu.VMEM),
            scratch_shapes=[
                pltpu.VMEM((chunks, channels, CHUNK_ROWS, cells), power.dtype),
                pltpu.VMEM((cores, chips, rows, width), f32),
                pltpu.VMEM((chips, rows, width), f32),
                pltpu.VMEM((chips, rows, width), f32),
                pltpu.VMEM((chips - 1, rows, width), f32),
                pltpu.VMEM((rows, width), f32),
                pltpu.VMEM((2, intervals, group, LANES), f32),
                pltpu.VMEM((2, intervals, group, LANES), f32),
                pltpu.SemaphoreType.DMA((chunks,)),
                pltpu.SemaphoreType.DMA((chunks,)),
                pltpu.SemaphoreType.DMA((chunks,)),
                pltpu.SemaphoreType.DMA((chips - 1, chunks)),
                pltpu.SemaphoreType.DMA((chips - 1, chunks)),
                pltpu.SemaphoreType.DMA((2, intervals)),
                pltpu.SemaphoreType.DMA((2, intervals)),
            ],
            compiler_params=pltpu.CompilerParams(collective_id=0, has_side_effects=True),
        )(window, calib_index, calib_table, power)

    return jax.shard_map(
        body,
        mesh=mesh,
        in_specs=(
            P(None, ("groups", "chan", "sub"), "dop", None),
            P("groups", None),
            P("groups", ("chan", "sub")),
            P(),
        ),
        out_specs=P(None, ("groups", "dop"), ("chan", "sub")),
        check_vma=False,
    )
```

time: 62.1 us -> 19.2 us (0.31)
  waiting for transfers between devices: 30.9 us -> 0 us
  Pallas kernels: 0 us -> 17.6 us
  between operations: 13.5 us -> 0.01 us
  starting transfers between devices: 7.68 us -> 0 us
  other arithmetic: 6.55 us -> 0 us
  matrix products: 1.87 us -> 0 us
    reduce_scatter x1 -> x0, waiting for transfers between devices: 29.9 us -> none  [body(): lax.psum_scatter(partial_sum, ('chan', 'sub'), scatter_dimension=2, tiled...]
    pallas_call x0 -> x1, Pallas kernels: none -> 17.6 us  [body(): pl.pallas_call(functools.partial(kernel, chips, cores), out_shape=jax.Sha...]
    ppermute x2 -> x0, starting transfers between devices: 7.68 us -> none  [the longest x1 5.76 us: extended(): lax.ppermute(lax.slice_in_dim(block, 0, width, axis=dim), axis, backward)]
    reduce_sum x2 -> x0, other arithmetic: 6.44 us -> none  [the longest x1 6.29 us: body(): partial_sum = jnp.sum(power, axis=1, dtype=jnp.float32)]
    dot_general x1 -> x0, matrix products: 1.87 us -> none  [body(): jnp.einsum('cdj,cji->cdi', padded, band_matrix, precision=lax.Precision.H...]
    unnamed x6 -> x1, local copies, waits for them, and re-layouts: 0.01 us -> 1.47 us
    slice x2 -> x0, local copies, waits for them, and re-layouts: 1.16 us -> none  [the longest x1 0.99 us: extended(): lax.slice_in_dim(block, block.shape[dim] - width, None, axis=dim)]
    ppermute x2 -> x0, waiting for transfers between devices: 0.97 us -> none  [the longest x1 0.97 us: extended(): lax.ppermute(lax.slice_in_dim(block, block.shape[dim] - width, None, axis...]
  transfers between devices with their start and end apart: 3 -> 0, of which waited for: 2 -> 0; matrix products, arithmetic and copies ran while one was open for 1% -> 0% of each run, Pallas kernels for 0% -> 0%
where the time goes in v1:
time: 19.2 us; the launch traced here: 19 us
  Pallas kernels  17.6 us (92%)
  local copies, waits for them, and re-layouts  1.47 us (8%)
    pallas_call x1, Pallas kernels, body(): pl.pallas_call(functools.partial(kernel, chips, cores), out_shape=jax.Sha...  17.6 us
    unnamed x1, local copies, waits for them, and re-layouts  1.47 us

profile of v1, /device:TPU:1, one launch (start us, length us, event | category | flops | bytes accessed | tf_op | source)
XLA Modules:
  0.0 19.0 jit_solution(5930001939765729263)
XLA Ops:
  0.0 17.6 %shard_map.46 = f32[2,64,128]{2,1,0:T(8,128)} custom-call(s32[2,2]{1,0:T(2,128)} %window.1, s32[2,4]{1,0:T(2,128)} %index.1, f32[16]{0:T(128)} %table.1, bf16[2,32,64,1024]{3,2,1,0:T(8,128)(2,1)} %power.1), custom_call_target="tpu_custom_call" | custom-call | tf_op jit(solution)/shard_map/pallas_call | solution.py:221
  17.6 1.5 %copy.6 = f32[2,64,128]{2,1,0:T(8,128)} copy(f32[2,64,128]{2,1,0:T(8,128)} %shard_map.46) | data formatting | bytes 131072

commit v2 on v1

--- a/solution.py
+++ b/solution.py
@@ -11,6 +11,7 @@
 CALIB = 32
 LANES = 128
 CHUNK_ROWS = 32
+VMEM_LIMIT = 60 * 2**20
 MESH = pl.DeviceIdType.MESH
 
 
@@ -24,7 +25,8 @@
 
 
 def kernel(
-    chips, cores, window, index, table, power, out,
+    chips, cores, window_in, index_in, table_in, power, top, bottom,
+    window, index, table, small_sem,
     raw, part, pair, total, inbox, strip, pack, halo,
     raw_sem, pair_send, pair_recv, z_send, z_recv, halo_send, halo_recv,
 ):
@@ -48,6 +50,15 @@
     for k in range(chunks):
         load(k).start()
 
+    small = [
+        pltpu.make_async_copy(source, target, small_sem.at[i])
+        for i, (source, target) in enumerate(
+            ((window_in, window), (index_in, index), (table_in, table))
+        )
+    ]
+    for copy in small:
+        copy.start()
+
     barrier = pltpu.get_barrier_semaphore()
 
     @pl.loop(1, strips)
@@ -62,7 +73,7 @@
         return pl.ds(k * CHUNK_ROWS, CHUNK_ROWS)
 
     def channel_sum(k):
-        @pl.loop(0, chips)
+        @pl.loop(0, chips, unroll=True)
         def _(j):
             for s in range(cores):
                 lanes = pl.ds(pl.multiple_of((j * cores + s) * cells, cells), cells)
@@ -70,12 +81,12 @@
                 for ch in range(channels):
                     x = raw[k, ch, :, lanes].astype(jnp.float32)
                     acc[ch % 2] = x if acc[ch % 2] is None else acc[ch % 2] + x
-                part[s, j, rows_of(k), :] = acc[0] + acc[1]
+                part[s, k, j] = acc[0] + acc[1]
 
     def to_pair(k):
         return pltpu.make_async_remote_copy(
-            src_ref=part.at[other, :, rows_of(k), :],
-            dst_ref=pair.at[:, rows_of(k), :],
+            src_ref=part.at[other, k],
+            dst_ref=pair.at[k],
             send_sem=pair_send.at[k],
             recv_sem=pair_recv.at[k],
             device_id={"sub": other},
@@ -89,8 +100,8 @@
         hop = offset(step)
         goal = lax.rem(chan + hop, chips)
         return pltpu.make_async_remote_copy(
-            src_ref=total.at[goal, rows_of(k), :],
-            dst_ref=inbox.at[hop - 1, rows_of(k), :],
+            src_ref=total.at[k, goal],
+            dst_ref=inbox.at[hop - 1, k],
             send_sem=z_send.at[hop - 1, k],
             recv_sem=z_recv.at[hop - 1, k],
             device_id={"chan": goal},
@@ -100,7 +111,7 @@
     def from_pair(k):
         to_pair(k).wait_recv()
         for j in range(chips):
-            total[j, rows_of(k), :] = part[sub, j, rows_of(k), :] + pair[j, rows_of(k), :]
+            total[k, j] = part[sub, k, j] + pair[k, j]
         for step in range(1, chips):
             to_owner(k, step).start()
 
@@ -123,9 +134,9 @@
         for k in range(c * per, (c + 1) * per):
             for hop in range(1, chips):
                 to_owner(k, hop).wait_recv()
-            value = total[chan, rows_of(k), :]
+            value = total[k, chan]
             for hop in range(1, chips):
-                value = value + inbox[hop - 1, rows_of(k), :]
+                value = value + inbox[hop - 1, k]
             strip[rows_of(k), :] = value
         for side in range(2):
             packed = None
@@ -157,6 +168,8 @@
     cell = lax.broadcasted_iota(jnp.int32, (1, LANES), 1)
     full_lane = lax.broadcasted_iota(jnp.int32, (dops, LANES), 1)
 
+    for copy in small:
+        copy.wait()
     bands, gains = [], []
     for c in range(intervals):
         guard, reach = window[c, 0], window[c, 1]
@@ -195,7 +208,8 @@
         window_sum = split_dot(jnp.concatenate([mine, edge], axis=1), bands[c])
         scale, count = gains[c]
         noise = window_sum / count
-        out[c] = mine / (scale * noise)
+        top[c] = mine
+        bottom[c] = scale * noise
 
     for k in range(chunks):
         to_pair(k).wait_send()
@@ -218,18 +232,21 @@
         chunks = rows // CHUNK_ROWS
         group = dops * HALO // LANES
         f32 = jnp.float32
-        return pl.pallas_call(
+        top, bottom = pl.pallas_call(
             functools.partial(kernel, chips, cores),
-            out_shape=jax.ShapeDtypeStruct((intervals, dops, width), f32),
-            in_specs=[pl.BlockSpec(memory_space=pltpu.SMEM)] * 3
-            + [pl.BlockSpec(memory_space=pl.ANY)],
-            out_specs=pl.BlockSpec(memory_space=pltpu.VMEM),
+            out_shape=[pltpu.VMEM((intervals, dops, width), f32)] * 2,
+            in_specs=[pl.BlockSpec(memory_space=pltpu.HBM)] * 4,
+            out_specs=[pl.BlockSpec(memory_space=pltpu.VMEM)] * 2,
             scratch_shapes=[
+                pltpu.SMEM(window.shape, window.dtype),
+                pltpu.SMEM(calib_index.shape, calib_index.dtype),
+                pltpu.SMEM(calib_table.shape, calib_table.dtype),
+                pltpu.SemaphoreType.DMA((3,)),
                 pltpu.VMEM((chunks, channels, CHUNK_ROWS, cells), power.dtype),
-                pltpu.VMEM((cores, chips, rows, width), f32),
-                pltpu.VMEM((chips, rows, width), f32),
-                pltpu.VMEM((chips, rows, width), f32),
-                pltpu.VMEM((chips - 1, rows, width), f32),
+                pltpu.VMEM((cores, chunks, chips, CHUNK_ROWS, width), f32),
+                pltpu.VMEM((chunks, chips, CHUNK_ROWS, width), f32),
+                pltpu.VMEM((chunks, chips, CHUNK_ROWS, width), f32),
+                pltpu.VMEM((chips - 1, chunks, CHUNK_ROWS, width), f32),
                 pltpu.VMEM((rows, width), f32),
                 pltpu.VMEM((2, intervals, group, LANES), f32),
                 pltpu.VMEM((2, intervals, group, LANES), f32),
@@ -241,8 +258,11 @@
                 pltpu.SemaphoreType.DMA((2, intervals)),
                 pltpu.SemaphoreType.DMA((2, intervals)),
             ],
-            compiler_params=pltpu.CompilerParams(collective_id=0, has_side_effects=True),
+            compiler_params=pltpu.CompilerParams(
+                collective_id=0, has_side_effects=True, vmem_limit_bytes=VMEM_LIMIT
+            ),
         )(window, calib_index, calib_table, power)
+        return top / bottom
 
     return jax.shard_map(
         body,

time: 19.2 us -> 16.9 us (0.88)
  Pallas kernels: 17.6 us -> 16.1 us
  local copies, waits for them, and re-layouts: 1.47 us -> 0 us
  other arithmetic: 0 us -> 0.65 us
    unnamed x1 -> x0, local copies, waits for them, and re-layouts: 1.47 us -> none
    pallas_call x1, Pallas kernels: 17.6 us -> 16.1 us  [body(): pl.pallas_call(functools.partial(kernel, chips, cores), out_shape=[pltpu....]
    div x0 -> x1, other arithmetic: none -> 0.65 us  [body(): return top / bottom]
where the time goes in v2:
time: 16.9 us; the launch traced here: 16.7 us
  Pallas kernels  16.1 us (95%)
  other arithmetic  0.65 us (4%)
    pallas_call x1, Pallas kernels, body(): pl.pallas_call(functools.partial(kernel, chips, cores), out_shape=[pltpu....  16.1 us
    div x1, other arithmetic, body(): return top / bottom  0.65 us

profile of v2, /device:TPU:1, one launch (start us, length us, event | category | flops | bytes accessed | tf_op | source)
XLA Modules:
  0.0 16.7 jit_solution(9722778568910740315)
XLA Ops:
  0.0 16.1 %shard_map.46 = (f32[2,64,128]{2,1,0:T(8,128)S(1)}, f32[2,64,128]{2,1,0:T(8,128)S(1)}) custom-call(s32[2,2]{1,0:T(2,128)} %window_in.1, s32[2,4]{1,0:T(2,128)} %index_in.1, f32[16]{0:T(128)} %table_in.1, bf16[2,32,64,1024]{3,2,1,0:T(8,128)(2,1)} %power.1), custom_call_target="tpu_custom_call" | custom-call | tf_op jit(solution)/shard_map/pallas_call | solution.py:235
  16.1 0.6 %div.3 = f32[2,64,128]{2,1,0:T(8,128)} divide(f32[2,64,128]{2,1,0:T(8,128)S(1)} %get-tuple-element.7, f32[2,64,128]{2,1,0:T(8,128)S(1)} %get-tuple-element.8) | non-fusion elementwise | flops 16384 | bytes 196608 | tf_op jit(solution)/shard_map/div | solution.py:265
